TPU v7x, 32 devices: a whole 2x2x4 slice. The times are simulated.
32 devices in a mesh: row: 4 (over y, x), col: 8 (over z, core).
Axes of the slice: x: 2, y: 2, z: 4, core: 2. Of those that a mesh axis runs over, the one named last changes fastest.
Arguments:
- layer_input: bfloat16 [8192, 2048], P(('row', 'col')), may hold values from -6 to 6
- out_grad: bfloat16 [8192, 2048], P(('row', 'col')), may hold values from -6 to 6
- kv_grad: bfloat16 [8192, 256], P(('row', 'col')), may hold values from -6 to 6
- lengths: int32 [4, 4], P('row'), may hold values from 1 to 1024, 2048 in all within a row
- token_deal: int32 [4, 2048], P('row'), may hold values from 0 to 2047, each once within a row
- attn_gain: float32 [2048], P('row'), may hold values from 0.25 to 1.75
- query_weight: float32 [2048, 2048], P('row', 'col'), may hold values from -0.125 to 0.125
- key_weight: float32 [2048, 128], P('row'), may hold values from -0.125 to 0.125
- value_weight: float32 [2048, 128], P('row'), may hold values from -0.125 to 0.125
- out_weight: float32 [2048, 2048], P('col', 'row'), may hold values from -1 to 1
- mlp_gain: float32 [2048], P('row'), may hold values from 0.25 to 1.75
- gate_weight: float32 [2048, 5632], P('row', 'col'), may hold values from -0.125 to 0.125
- up_weight: float32 [2048, 5632], P('row', 'col'), may hold values from -0.125 to 0.125
- down_weight: float32 [5632, 2048], P('col', 'row'), may hold values from -0.3125 to 0.3125
Outputs:
- layer_output: bfloat16 [8192, 2048], P(('row', 'col'))
- input_grad: float32 [8192, 2048], P(('row', 'col'))
- shared_kv: bfloat16 [8192, 256], P(('row', 'col'))
- attn_gain_grad: float32 [2048], P('row')
- query_weight_grad: float32 [2048, 2048], P('row', 'col')
- key_weight_grad: float32 [2048, 128], P('row')
- value_weight_grad: float32 [2048, 128], P('row')
- out_weight_grad: float32 [2048, 2048], P('col', 'row')
- mlp_gain_grad: float32 [2048], P('row')
- gate_weight_grad: float32 [2048, 5632], P('row', 'col')
- up_weight_grad: float32 [2048, 5632], P('row', 'col')
- down_weight_grad: float32 [5632, 2048], P('col', 'row')
Inputs may be any that keep to these rules, and one draw needn't show every extreme that they name: Each row holds 4 lengths that sum to 2048; the longest of each row is exactly 1024. `token_deal`: each row is a permutation of 0 to 2047.
All inputs are finite; a program needn't handle non-finite values.
Results may differ from a plain program's by a relative error of at most 0.017.
The roundings to bfloat16 on the way count: a program that leaves them out, or rounds other values in their place, can miss the bound.
Values may be sent and summed in bfloat16 or wider, within the bound.
No kernel may reach another device: no remote copies, remote signals or barrier semaphores. Data moves between devices by JAX's collectives and lax.ppermute only.
A program may use at most 320 MiB of HBM per device.

v0:
```python
import jax
import jax.numpy as jnp
from jax import lax
from jax.sharding import PartitionSpec as P

norm_eps = 1e-05
rope_base = 10000.0
masked_score = -1e30


def rotate_pairs(values, positions, direction):
    half_dim = values.shape[-1] // 2
    frequency = rope_base ** (-jnp.arange(half_dim, dtype=jnp.float32) / half_dim)
    angles = positions.astype(jnp.float32)[:, None, None] * frequency
    cosine = jnp.cos(angles)
    sine_part = jnp.sin(angles) * direction
    first_half = values[..., :half_dim]
    second = values[..., half_dim:]
    return jnp.concatenate(
        [first_half * cosine - second * sine_part, second * cosine + first_half * sine_part],
        axis=-1,
    )


def norm_parts(values, gain):
    factor = lax.rsqrt(jnp.mean(values * values, axis=-1, keepdims=True) + norm_eps)
    return (factor, values * factor * gain)


def norm_backward(values, factor, gain, grad_rows):
    weighted = grad_rows * gain
    inner_mean = jnp.mean(weighted * values, axis=-1, keepdims=True)
    input_part = factor * weighted - values * factor * factor * factor * inner_mean
    gain_part = jnp.sum(grad_rows * values * factor, axis=0)
    return (input_part, gain_part)


def sequence_info(seq_lengths, group_rows):
    positions = jnp.arange(group_rows, dtype=jnp.int32)
    seq_ends = jnp.cumsum(seq_lengths)
    seq_ids = jnp.sum((positions[:, None] >= seq_ends[None, :]).astype(jnp.int32), axis=1)
    starts = jnp.sum(
        jnp.where(seq_ends[None, :] <= positions[:, None], seq_lengths[None, :], 0), axis=1
    )
    return (positions, seq_ids, positions - starts)


def block_scores(query_block, key_rows, seq_ids, first_row, block_rows, score_scale):
    key_index = jnp.arange(key_rows.shape[0], dtype=jnp.int32)
    row_index = first_row + jnp.arange(block_rows, dtype=jnp.int32)
    row_seq = lax.dynamic_slice_in_dim(seq_ids, first_row, block_rows, 0)
    scores = (
        jnp.einsum("qhd,kd->hqk", query_block, key_rows, preferred_element_type=jnp.float32)
        * score_scale
    )
    allowed = (row_seq[:, None] == seq_ids[None, :]) & (key_index[None, :] <= row_index[:, None])
    return jnp.where(allowed[None], scores, masked_score)


def attend_forward(queries, key_rows, value_rows, seq_ids):
    group_rows, head_count, head_dim = queries.shape
    block_rows = min(512, group_rows)
    score_scale = float(head_dim) ** (-0.5)
    count_blocks = group_rows // block_rows
    query_blocks = queries.reshape(count_blocks, block_rows, head_count, head_dim)
    first_rows = jnp.arange(count_blocks, dtype=jnp.int32) * block_rows

    def one_block(pieces):
        query_block, first_row = pieces
        scores = block_scores(query_block, key_rows, seq_ids, first_row, block_rows, score_scale)
        highest = jnp.max(scores, axis=-1, keepdims=True)
        exponent = jnp.exp(scores - highest)
        row_total = jnp.sum(exponent, axis=-1, keepdims=True)
        prob_low = (exponent / row_total).astype(jnp.bfloat16)
        mixed_rows = jnp.einsum(
            "hqk,kd->qhd", prob_low, value_rows, preferred_element_type=jnp.float32
        )
        return (mixed_rows.astype(jnp.bfloat16), (highest + jnp.log(row_total))[..., 0])

    mixed_rows, log_norm = lax.map(one_block, (query_blocks, first_rows))
    return (mixed_rows.reshape(group_rows, head_count, head_dim), log_norm)


def attend_backward(queries, key_rows, value_rows, seq_ids, mixed_grad, log_norm):
    group_rows, head_count, head_dim = queries.shape
    block_rows = min(512, group_rows)
    score_scale = float(head_dim) ** (-0.5)
    count_blocks = group_rows // block_rows
    query_blocks = queries.reshape(count_blocks, block_rows, head_count, head_dim)
    grad_blocks = mixed_grad.reshape(count_blocks, block_rows, head_count, head_dim)
    first_rows = jnp.arange(count_blocks, dtype=jnp.int32) * block_rows

    def one_block(carry, pieces):
        key_grad, value_grad = carry
        query_block, grad_block, norm_block, first_row = pieces
        scores = block_scores(query_block, key_rows, seq_ids, first_row, block_rows, score_scale)
        softmax_rows = jnp.exp(scores - norm_block[..., None])
        prob_low = softmax_rows.astype(jnp.bfloat16)
        prob_grad = jnp.einsum(
            "qhd,kd->hqk", grad_block, value_rows, preferred_element_type=jnp.float32
        )
        row_dot = jnp.sum(softmax_rows * prob_grad, axis=-1, keepdims=True)
        score_grad = (softmax_rows * (prob_grad - row_dot)).astype(jnp.bfloat16)
        query_grad = (
            jnp.einsum("hqk,kd->qhd", score_grad, key_rows, preferred_element_type=jnp.float32)
            * score_scale
        )
        key_grad = (
            key_grad
            + jnp.einsum("hqk,qhd->kd", score_grad, query_block, preferred_element_type=jnp.float32)
            * score_scale
        )
        value_grad = value_grad + jnp.einsum(
            "hqk,qhd->kd", prob_low, grad_block, preferred_element_type=jnp.float32
        )
        return ((key_grad, value_grad), query_grad)

    zero_rows = jnp.zeros((group_rows, head_dim), jnp.float32)
    (key_grad, value_grad), query_grad = lax.scan(
        one_block, (zero_rows, zero_rows), (query_blocks, grad_blocks, log_norm, first_rows)
    )
    return (query_grad.reshape(group_rows, head_count, head_dim), key_grad, value_grad)


def local(
    layer_input,
    out_grad,
    kv_grad,
    lengths,
    token_deal,
    attn_gain,
    query_weight,
    key_weight,
    value_weight,
    out_weight,
    mlp_gain,
    gate_weight,
    up_weight,
    down_weight,
):
    own_rows = layer_input.shape[0]
    col_index = lax.axis_index("col")
    group_rows = own_rows * lax.axis_size("col")
    head_dim = key_weight.shape[1]
    (
        gain_one,
        query_copy,
        key_copy,
        value_copy,
        out_copy,
        gain_two,
        gate_copy,
        up_copy,
        down_copy,
    ) = (
        lax.all_gather(attn_gain.astype(jnp.bfloat16), "row", axis=0, tiled=True),
        lax.all_gather(query_weight.astype(jnp.bfloat16), "row", axis=0, tiled=True),
        lax.all_gather(key_weight.astype(jnp.bfloat16), "row", axis=0, tiled=True),
        lax.all_gather(value_weight.astype(jnp.bfloat16), "row", axis=0, tiled=True),
        lax.all_gather(out_weight.astype(jnp.bfloat16), "row", axis=1, tiled=True),
        lax.all_gather(mlp_gain.astype(jnp.bfloat16), "row", axis=0, tiled=True),
        lax.all_gather(gate_weight.astype(jnp.bfloat16), "row", axis=0, tiled=True),
        lax.all_gather(up_weight.astype(jnp.bfloat16), "row", axis=0, tiled=True),
        lax.all_gather(down_weight.astype(jnp.bfloat16), "row", axis=1, tiled=True),
    )
    gain_one = gain_one.astype(jnp.float32)
    gain_two = gain_two.astype(jnp.float32)
    head_count = query_copy.shape[1] // head_dim
    positions, seq_ids, within = sequence_info(lengths[0], group_rows)
    slot_order = token_deal[0]
    inverse = jnp.zeros((group_rows,), jnp.int32).at[slot_order].set(positions)
    slot_pos = within[slot_order]
    own_pos = lax.dynamic_slice_in_dim(slot_pos, col_index * own_rows, own_rows, 0)
    input_rows = layer_input.astype(jnp.float32)
    factor_one, normed_one = norm_parts(input_rows, gain_one)
    normed_own = normed_one.astype(jnp.bfloat16)
    normed_rows, grad_rows = (
        lax.all_gather(normed_own, "col", axis=0, tiled=True),
        lax.all_gather(out_grad, "col", axis=0, tiled=True),
    )
    queries = jnp.dot(normed_rows, query_copy, preferred_element_type=jnp.float32).reshape(
        group_rows, head_count, head_dim
    )
    queries = rotate_pairs(queries, slot_pos, 1.0).astype(jnp.bfloat16)
    key_proj = jnp.dot(normed_rows, key_copy, preferred_element_type=jnp.float32)
    key_rows = rotate_pairs(key_proj[:, None, :], slot_pos, 1.0)[:, 0, :].astype(jnp.bfloat16)
    value_rows = jnp.dot(normed_rows, value_copy, preferred_element_type=jnp.float32).astype(
        jnp.bfloat16
    )
    shared_rows = jnp.concatenate([key_rows, value_rows], axis=1)
    shared_own = lax.dynamic_slice_in_dim(shared_rows, col_index * own_rows, own_rows, 0)
    query_orig = queries[inverse]
    key_orig = key_rows[inverse]
    value_orig = value_rows[inverse]
    mixed_orig, log_norm = attend_forward(query_orig, key_orig, value_orig, seq_ids)
    mixed_slot = mixed_orig[slot_order].reshape(group_rows, head_count * head_dim)
    out_full = lax.all_gather(out_copy, "col", axis=0, tiled=True)
    mixed_own = lax.all_to_all(mixed_slot, "col", split_axis=0, concat_axis=1, tiled=True)
    attended = jnp.dot(mixed_own, out_full, preferred_element_type=jnp.float32)
    middle = input_rows + attended
    factor_two, normed_two = norm_parts(middle, gain_two)
    mlp_rows = lax.all_gather(normed_two.astype(jnp.bfloat16), "col", axis=0, tiled=True)
    gate_act = jnp.dot(mlp_rows, gate_copy, preferred_element_type=jnp.float32)
    upward = jnp.dot(mlp_rows, up_copy, preferred_element_type=jnp.float32)
    sigmoid_gate = jax.nn.sigmoid(gate_act)
    silu_gate = gate_act * sigmoid_gate
    hidden = (silu_gate * upward).astype(jnp.bfloat16)
    output_rows = middle + lax.psum_scatter(
        jnp.dot(hidden, down_copy, preferred_element_type=jnp.float32),
        "col",
        scatter_dimension=0,
        tiled=True,
    )
    hidden_grad = jnp.dot(grad_rows, down_copy.T, preferred_element_type=jnp.float32)
    down_wgrad = jnp.dot(hidden.T, grad_rows, preferred_element_type=jnp.float32)
    gate_grad = (
        hidden_grad * upward * sigmoid_gate * (1.0 + gate_act * (1.0 - sigmoid_gate))
    ).astype(jnp.bfloat16)
    up_grad = (hidden_grad * silu_gate).astype(jnp.bfloat16)
    gate_wgrad = jnp.dot(mlp_rows.T, gate_grad, preferred_element_type=jnp.float32)
    up_wgrad = jnp.dot(mlp_rows.T, up_grad, preferred_element_type=jnp.float32)
    normed_two_grad = lax.psum_scatter(
        jnp.dot(gate_grad, gate_copy.T, preferred_element_type=jnp.float32)
        + jnp.dot(up_grad, up_copy.T, preferred_element_type=jnp.float32),
        "col",
        scatter_dimension=0,
        tiled=True,
    )
    middle_part, gain_two_grad = norm_backward(middle, factor_two, gain_two, normed_two_grad)
    middle_grad = out_grad.astype(jnp.float32) + middle_part
    middle_low = middle_grad.astype(jnp.bfloat16)
    middle_rows = lax.all_gather(middle_low, "col", axis=0, tiled=True)
    mixed_grad_slot = jnp.dot(middle_rows, out_copy.T, preferred_element_type=jnp.float32).astype(
        jnp.bfloat16
    )
    out_wgrad = jnp.dot(mixed_slot.T, middle_rows, preferred_element_type=jnp.float32)
    mixed_grad = mixed_grad_slot.reshape(group_rows, head_count, head_dim)[inverse]
    query_grad, key_grad, value_grad = attend_backward(
        query_orig, key_orig, value_orig, seq_ids, mixed_grad, log_norm
    )
    query_grad = (
        rotate_pairs(query_grad[slot_order], slot_pos, -1.0)
        .astype(jnp.bfloat16)
        .reshape(group_rows, head_count * head_dim)
    )
    query_wgrad = jnp.dot(normed_rows.T, query_grad, preferred_element_type=jnp.float32)
    shared_part = jnp.concatenate([key_grad, value_grad], axis=1)[slot_order]
    shared_cols = shared_part.shape[1]
    grad_parts = jnp.concatenate(
        [jnp.dot(query_grad, query_copy.T, preferred_element_type=jnp.float32), shared_part], axis=1
    )
    summed_parts = lax.psum_scatter(grad_parts, "col", scatter_dimension=0, tiled=True)
    width_cols = summed_parts.shape[1] - shared_cols
    normed_one_grad = summed_parts[:, :width_cols]
    shared_grad = summed_parts[:, width_cols:]
    shared_grad = shared_grad + kv_grad.astype(jnp.float32)
    key_own = rotate_pairs(shared_grad[:, None, :head_dim], own_pos, -1.0)[:, 0, :].astype(
        jnp.bfloat16
    )
    value_own = shared_grad[:, head_dim:].astype(jnp.bfloat16)
    key_wgrad = jnp.dot(normed_own.T, key_own, preferred_element_type=jnp.float32)
    value_wgrad = jnp.dot(normed_own.T, value_own, preferred_element_type=jnp.float32)
    normed_one_grad = (
        normed_one_grad
        + jnp.dot(key_own, key_copy.T, preferred_element_type=jnp.float32)
        + jnp.dot(value_own, value_copy.T, preferred_element_type=jnp.float32)
    )
    input_part, gain_one_grad = norm_backward(input_rows, factor_one, gain_one, normed_one_grad)
    input_grad = middle_grad + input_part
    summed = (
        lax.psum_scatter(gain_one_grad, "row", scatter_dimension=0, tiled=True),
        lax.psum_scatter(query_wgrad, "row", scatter_dimension=0, tiled=True),
        lax.psum_scatter(key_wgrad, "row", scatter_dimension=0, tiled=True),
        lax.psum_scatter(value_wgrad, "row", scatter_dimension=0, tiled=True),
        lax.psum_scatter(out_wgrad, "row", scatter_dimension=1, tiled=True),
        lax.psum_scatter(gain_two_grad, "row", scatter_dimension=0, tiled=True),
        lax.psum_scatter(gate_wgrad, "row", scatter_dimension=0, tiled=True),
        lax.psum_scatter(up_wgrad, "row", scatter_dimension=0, tiled=True),
        lax.psum_scatter(down_wgrad, "row", scatter_dimension=1, tiled=True),
    )
    gain_one_sum, key_sum, value_sum, gain_two_sum = lax.psum(
        (summed[0], summed[2], summed[3], summed[5]), "col"
    )
    return (
        output_rows.astype(jnp.bfloat16),
        input_grad,
        shared_own,
        gain_one_sum,
        summed[1],
        key_sum,
        value_sum,
        summed[4],
        gain_two_sum,
        summed[6],
        summed[7],
        summed[8],
    )


def solution(mesh):
    in_specs = (
        P(("row", "col"), None),
        P(("row", "col"), None),
        P(("row", "col"), None),
        P("row", None),
        P("row", None),
        P("row"),
        P("row", "col"),
        P("row", None),
        P("row", None),
        P("col", "row"),
        P("row"),
        P("row", "col"),
        P("row", "col"),
        P("col", "row"),
    )
    out_specs = (
        P(("row", "col"), None),
        P(("row", "col"), None),
        P(("row", "col"), None),
        P("row"),
        P("row", "col"),
        P("row", None),
        P("row", None),
        P("col", "row"),
        P("row"),
        P("row", "col"),
        P("row", "col"),
        P("col", "row"),
    )
    return jax.shard_map(local, mesh=mesh, in_specs=in_specs, out_specs=out_specs, check_vma=False)
```

profile of v0, /device:TPU:0, one launch (start us, length us, event | category | flops | bytes accessed | tf_op | source)
XLA Modules:
  0.0 1775.5 jit_solution(17734194517630113278)
XLA Ops:
  9.8 9.6 all-gather
  24.0 15.5 all-gather.17.cloned.1.call-done
  40.9 8.0 scatter_custom_fusion
  49.1 11.8 gather_fusion
  61.0 10.1 all_gather.46
  71.1 9.6 all_gather.45
  86.4 37.8 %all-gather.13.cloned.1.call-done = bf16[2048,2048]{0,1:T(8,128)(2,1)} async-done(((bf16[256,2048]{0,1:T(8,128)(2,1)}), bf16[2048,2048]{0,1:T(8,128)(2,1)}) %all-gather.13.cloned.1.call-update) | async-done | bytes 8388624 | tf_op jit(solution)/shard_map/all_gather | solution.py:178
  137.6 6.2 gather_fusion.3
  173.8 13.9 gather_fusion.1
  189.1 50.7 %while.27 = (s32[]{:T(128)}, bf16[4,512,2,128]{3,1,0,2:T(8,128)(2,1)}, f32[4,2,512]{2,1,0:T(2,128)S(1)}, s32[4]{0:T(128)S(1)}, s32[2048]{0:T(1024)S(1)}, /*index...) while((s32[]{:T(128)}, ...), condition=%wide.region_8.9_spmd, body=%wide.region_5.8_spmd.sunk | while | flops 1102183936 | bytes 30984376 | solution.py:80
  243.9 15.1 gather_fusion.4
  268.5 8.2 all-gather.1
  276.7 18.2 %all-to-all-done = bf16[8,256,256]{1,2,0:T(8,128)(2,1)S(1)} async-done(((bf16[8,256,256]{1,2,0:T(8,128)(2,1)}), bf16[8,256,256]{1,2,0:T(8,128)(2,1)S(1)}, u32[]{:S(2)}, u32[]{:S(2)}) %all-to-all-start) | async-done | bytes 1048608 | tf_op jit(solution)/shard_map/all_to_all | solution.py:198
  295.9 7.1 multiply_reduce_fusion.2
  310.7 74.6 %all-gather.21.cloned.1.call-done = bf16[2048,2048]{0,1:T(8,128)(2,1)} async-done(((bf16[256,2048]{0,1:T(8,128)(2,1)}), bf16[2048,2048]{0,1:T(8,128)(2,1)}) %all-gather.21.cloned.1.call-update) | async-done | bytes 8388624 | tf_op jit(solution)/shard_map/all_gather | solution.py:202
  385.3 11.0 fusion.99
  396.3 31.1 %all-gather.25.cloned.1.call-done = bf16[2048,704]{0,1:T(8,128)(2,1)} async-done(((bf16[512,704]{0,1:T(8,128)(2,1)}), bf16[2048,704]{0,1:T(8,128)(2,1)}) %all-gather.25.cloned.1.call-update) | async-done | bytes 2883600 | tf_op jit(solution)/shard_map/all_gather | solution.py:163
  427.4 11.0 fusion.100
  438.5 32.4 %all-gather.27.cloned.1.call-done = bf16[704,2048]{1,0:T(8,128)(2,1)} async-done(((bf16[704,512]{1,0:T(8,128)(2,1)}), bf16[704,2048]{1,0:T(8,128)(2,1)}) %all-gather.27.cloned.1.call-update) | async-done | bytes 2883600 | tf_op jit(solution)/shard_map/all_gather | solution.py:164
  470.8 83.7 %all-gather.29.cloned.1.call-done = bf16[2048,2048]{1,0:T(8,128)(2,1)} async-done(((bf16[256,2048]{1,0:T(8,128)(2,1)}), bf16[2048,2048]{1,0:T(8,128)(2,1)}) %all-gather.29.cloned.1.call-update) | async-done | bytes 8388624 | tf_op jit(solution)/shard_map/all_gather | solution.py:179
  554.5 15.3 multiply_convert_fusion
  569.8 10.4 fusion.94
  580.2 13.8 convolution_add_fusion
  595.7 165.2 %reduce-scatter.13.cloned.1.call-done = f32[256,2048]{0,1:T(8,128)} async-done(((f32[2048,2048]{0,1:T(8,128)}), f32[256,2048]{0,1:T(8,128)}) %reduce-scatter.13.cloned.1.call-update) | async-done | bytes 2097168 | tf_op jit(solution)/shard_map/reduce_scatter | solution.py:222
  765.8 81.0 %all-gather.31.cloned.1.call-done = bf16[2048,2048]{0,1:T(8,128)(2,1)} async-done(((bf16[256,2048]{0,1:T(8,128)(2,1)}), bf16[2048,2048]{0,1:T(8,128)(2,1)}) %all-gather.31.cloned.1.call-update) | async-done | bytes 8388624 | tf_op jit(solution)/shard_map/all_gather | solution.py:232
  846.8 7.0 convolution_convert_fusion
  857.8 15.1 gather_fusion.5
  873.0 77.5 %while.28 = (s32[]{:T(128)}, f32[2048,128]{1,0:T(8,128)S(1)}, f32[2048,128]{1,0:T(8,128)}, f32[4,512,2,128]{3,1,0,2:T(8,128)}, s32[4]{0:T(128)S(1)}, /*index=5*/...) while((s32[]{:T(128)}, f32[2048,128]{1,0:T(8,128)S(1)}, ...), condition=%wide.region_15.16_spmd.clone, body=%wide.region_13.15_spmd.clone.sunk | while | flops 2720398848 | bytes 83409176 | solution.py:119
  955.3 14.5 gather_fusion.6
  971.2 8.6 gather_fusion.7
  982.9 8.9 subtract_convert_fusion
  997.1 8.7 pad_maximum_fusion
  1007.6 184.5 %reduce-scatter.15.cloned.1.call-done = f32[256,2304]{0,1:T(8,128)} async-done(((f32[2048,2304]{0,1:T(8,128)}), f32[256,2304]{0,1:T(8,128)}) %reduce-scatter.15.cloned.1.call-update) | async-done | bytes 2359312 | tf_op jit(solution)/shard_map/reduce_scatter | solution.py:252
  1196.5 12.7 fusion.93
  1209.2 11.2 fusion.98
  1220.5 11.2 fusion.96
  1231.8 11.1 fusion.97
  1243.2 7.3 fusion.59
  1252.6 7.5 fusion.95
  1267.7 154.9 %reduce-scatter.11.cloned.1.call-done = f32[256,2048]{0,1:T(8,128)} async-done(((f32[2048,2048]{0,1:T(8,128)}), f32[256,2048]{0,1:T(8,128)}) %reduce-scatter.11.cloned.1.call-update) | async-done | bytes 2097168 | tf_op jit(solution)/shard_map/reduce_scatter | solution.py:208
  1427.5 17.1 all-reduce.4
  1449.1 14.2 all-reduce.2
  1463.3 27.2 %reduce-scatter.29.cloned.1.call-done = f32[704,512]{1,0:T(8,128)} async-done(((f32[704,2048]{1,0:T(8,128)}), f32[704,512]{1,0:T(8,128)}) %reduce-scatter.29.cloned.1.call-update) | async-done | bytes 1441808 | tf_op jit(solution)/shard_map/reduce_scatter | solution.py:279
  1490.4 69.1 %reduce-scatter.25.cloned.1.call-done = f32[512,704]{0,1:T(8,128)} async-done(((f32[2048,704]{0,1:T(8,128)}), f32[512,704]{0,1:T(8,128)}) %reduce-scatter.25.cloned.1.call-update) | async-done | bytes 1441808 | tf_op jit(solution)/shard_map/reduce_scatter | solution.py:277
  1559.5 69.1 %reduce-scatter.27.cloned.1.call-done = f32[512,704]{0,1:T(8,128)} async-done(((f32[2048,704]{0,1:T(8,128)}), f32[512,704]{0,1:T(8,128)}) %reduce-scatter.27.cloned.1.call-update) | async-done | bytes 1441808 | tf_op jit(solution)/shard_map/reduce_scatter | solution.py:278
  1628.7 38.8 %reduce-scatter.17.cloned.1.call-done = f32[512,256]{1,0:T(8,128)} async-done(((f32[2048,256]{1,0:T(8,128)}), f32[512,256]{1,0:T(8,128)}) %reduce-scatter.17.cloned.1.call-update) | async-done | bytes 524304 | tf_op jit(solution)/shard_map/reduce_scatter | solution.py:272
  1667.4 38.6 %reduce-scatter.23.cloned.1.call-done = f32[256,512]{1,0:T(8,128)} async-done(((f32[256,2048]{1,0:T(8,128)}), f32[256,512]{1,0:T(8,128)}) %reduce-scatter.23.cloned.1.call-update) | async-done | bytes 524304 | tf_op jit(solution)/shard_map/reduce_scatter | solution.py:275
  1706.0 59.0 %all-reduce.7.cloned.1.call-done = (f32[512,128]{1,0:T(8,128)}, f32[512,128]{1,0:T(8,128)}) async-done(((f32[512,128]{1,0:T(8,128)}, f32[512,128]{1,0:T(8,128)}), (f32[512,128]{1,0:T(8,128)}, f32[512,128]{1,0:T(8,128)})) %all-reduce.7.cloned.1.call-update) | async-done | bytes 524304 | tf_op jit(solution)/shard_map/psum | solution.py:281
  (345 shorter events, 246.1 us)
Async XLA Ops:
  7.2 32.3 %all-gather.17.cloned.1.call-start = ((), (), s32[]{:S(2)}) async-start(), calls=%async_computation.13 | async-start | bytes 1310720 | tf_op jit(solution)/shard_map/all_gather | solution.py:160
  9.0 115.2 %all-gather.13.cloned.1.call-start = ((), (), s32[]{:S(2)}) async-start(), calls=%async_computation.11 | async-start | bytes 9437184 | tf_op jit(solution)/shard_map/all_gather | solution.py:178
  20.9 275.0 %copy-start.2 = (bf16[256,2048]{0,1:T(8,128)(2,1)}, bf16[256,2048]{0,1:T(8,128)(2,1)S(1)}, u32[]{:S(2)}) copy-start(bf16[256,2048]{0,1:T(8,128)(2,1)S(1)} %copy.114) | copy-start | bytes 3145732
  21.2 18.3 %copy-start.26 = (f32[512,704]{0,1:T(8,128)S(1)}, f32[512,704]{0,1:T(8,128)}, u32[]{:S(2)}) copy-start(f32[512,704]{0,1:T(8,128)} %param.29) | copy-start | bytes 4325380
  23.2 128.1 %all-gather.15.cloned.1.call-start = ((), (), s32[]{:S(2)}) async-start(), calls=%async_computation.12 | async-start | bytes 1310720 | tf_op jit(solution)/shard_map/all_gather | solution.py:157
  24.0 252.7 %all-gather.19.cloned.1.call-start = ((), (), s32[]{:S(2)}) async-start(), calls=%async_computation.14 | async-start | bytes 9437184 | tf_op jit(solution)/shard_map/all_gather | solution.py:197
  39.5 271.1 %all-gather.23.cloned.1.call-start = ((), (), s32[]{:S(2)}) async-start(), calls=%async_computation.16 | async-start | bytes 3604480 | tf_op jit(solution)/shard_map/all_gather | solution.py:162
  40.6 93.5 %copy-start.52 = (f32[64]{0:T(128)}, f32[64]{0:T(128)S(1)}, u32[]{:S(2)}) copy-start(f32[64]{0:T(128)S(1)} %multiply_power_fusion) | copy-start | bytes 772
  48.9 124.8 %copy-start.36 = (s32[2048]{0:T(1024)}, s32[2048]{0:T(1024)S(1)}, u32[]{:S(2)}) copy-start(s32[2048]{0:T(1024)S(1)} %fusion.85) | copy-start | bytes 24580
  49.1 194.8 %copy-start.38 = (s32[2048]{0:T(1024)}, s32[2048]{0:T(1024)S(1)}, u32[]{:S(2)}) copy-start(s32[2048]{0:T(1024)S(1)} %get-tuple-element.398) | copy-start | bytes 24580
  60.9 68.0 %copy-start.43 = (s32[2048]{0:T(1024)}, s32[2048]{0:T(1024)S(1)}, u32[]{:S(2)}) copy-start(s32[2048]{0:T(1024)S(1)} %gather_fusion) | copy-start | bytes 24580
  71.1 53.1 %copy-start.25 = (bf16[2048,128]{1,0:T(8,128)(2,1)}, bf16[2048,128]{1,0:T(8,128)(2,1)S(1)}, u32[]{:S(2)}) copy-start(bf16[2048,128]{1,0:T(8,128)(2,1)S(1)} %all_gather.46) | copy-start | bytes 1572868
  80.6 48.6 %copy-start.21 = (bf16[2048,128]{1,0:T(8,128)(2,1)}, bf16[2048,128]{1,0:T(8,128)(2,1)S(1)}, u32[]{:S(2)}) copy-start(bf16[2048,128]{1,0:T(8,128)(2,1)S(1)} %all_gather.45) | copy-start | bytes 1572868
  239.8 21.7 %copy-start.4 = (bf16[2048,128]{1,0:T(8,128)(2,1)}, bf16[2048,128]{1,0:T(8,128)(2,1)S(1)}, u32[]{:S(2)}) copy-start(bf16[2048,128]{1,0:T(8,128)(2,1)S(1)} %get-tuple-element.636) | copy-start | bytes 1572868
  239.8 21.7 %copy-start.6 = (bf16[2048,128]{1,0:T(8,128)(2,1)}, bf16[2048,128]{1,0:T(8,128)(2,1)S(1)}, u32[]{:S(2)}) copy-start(bf16[2048,128]{1,0:T(8,128)(2,1)S(1)} %get-tuple-element.637) | copy-start | bytes 1572868
  239.8 21.7 %copy-start.11 = (bf16[4,512,2,128]{3,1,2,0:T(8,128)(2,1)}, bf16[4,512,2,128]{3,1,2,0:T(8,128)(2,1)S(1)}, u32[]{:S(2)}) copy-start(bf16[4,512,2,128]{3,1,2,0:T(8,128)(2,1)S(1)} %get-tuple-element.645) | copy-start | bytes 3145732
  263.8 31.2 %all-to-all-start = ((bf16[8,256,256]{1,2,0:T(8,128)(2,1)}), bf16[8,256,256]{1,2,0:T(8,128)(2,1)S(1)}, u32[]{:S(2)}, u32[]{:S(2)}) async-start(bf16[8,256,256]{1,2,0:T(8,128)(2,1)} %copy.124), calls=%async_computation | async-start | bytes 2097152 | tf_op jit(solution)/shard_map/all_to_all | solution.py:198
  268.4 116.9 %all-gather.21.cloned.1.call-start = ((), (), s32[]{:S(2)}) async-start(), calls=%async_computation.15 | async-start | bytes 9437184 | tf_op jit(solution)/shard_map/all_gather | solution.py:202
  276.7 487.3 %copy-start.34 = (f32[4,1,512]{2,1,0:T(1,128)}, f32[4,1,512]{2,1,0:T(1,128)S(1)}, u32[]{:S(2)}) copy-start(f32[4,1,512]{2,1,0:T(1,128)S(1)} %convert_element_type.144) | copy-start | bytes 24580
  303.0 460.9 %copy-start = (f32[256,2048]{0,1:T(8,128)}, f32[256,2048]{0,1:T(8,128)S(1)}, u32[]{:S(2)}) copy-start(f32[256,2048]{0,1:T(8,128)S(1)} %get-tuple-element.395) | copy-start | bytes 6291460
  303.1 460.9 %copy-start.45 = (f32[256]{0:T(256)}, f32[256]{0:T(256)S(1)}, u32[]{:S(2)}) copy-start(f32[256]{0:T(256)S(1)} %add_rsqrt_fusion) | copy-start | bytes 3076
  304.7 122.8 %all-gather.25.cloned.1.call-start = ((), (), s32[]{:S(2)}) async-start(), calls=%async_computation.17 | async-start | bytes 3604480 | tf_op jit(solution)/shard_map/all_gather | solution.py:163
  307.1 163.8 %all-gather.27.cloned.1.call-start = ((), (), s32[]{:S(2)}) async-start(), calls=%async_computation.18 | async-start | bytes 3604480 | tf_op jit(solution)/shard_map/all_gather | solution.py:164
  309.8 244.7 %all-gather.29.cloned.1.call-start = ((), (), s32[]{:S(2)}) async-start(), calls=%async_computation.20 | async-start | bytes 9437184 | tf_op jit(solution)/shard_map/all_gather | solution.py:179
  310.6 450.3 %reduce-scatter.13.cloned.1.call-start = ((), (), s32[]{:S(2)}) async-start(), calls=%async_computation.21 | async-start | bytes 18874368 | tf_op jit(solution)/shard_map/reduce_scatter | solution.py:222
  594.1 252.7 %all-gather.31.cloned.1.call-start = ((), (), s32[]{:S(2)}) async-start(), calls=%async_computation.22 | async-start | bytes 9437184 | tf_op jit(solution)/shard_map/all_gather | solution.py:232
  595.7 170.0 %copy-start.14 = (bf16[256,2048]{0,1:T(8,128)(2,1)}, bf16[256,2048]{0,1:T(8,128)(2,1)S(1)}, u32[]{:S(2)}) copy-start(bf16[256,2048]{0,1:T(8,128)(2,1)S(1)} %copy.127) | copy-start | bytes 3145732
  765.7 426.4 %reduce-scatter.15.cloned.1.call-start = ((), (), s32[]{:S(2)}) async-start(), calls=%async_computation.23 | async-start | bytes 21233664 | tf_op jit(solution)/shard_map/reduce_scatter | solution.py:252
  765.8 92.1 %copy-start.37 = (s32[2048]{0:T(1024)S(1)}, s32[2048]{0:T(1024)}, u32[]{:S(2)}) copy-start(s32[2048]{0:T(1024)} %copy-done.36) | copy-start | bytes 24580
  853.9 19.1 %copy-start.5 = (bf16[2048,128]{1,0:T(8,128)(2,1)S(1)}, bf16[2048,128]{1,0:T(8,128)(2,1)}, u32[]{:S(2)}) copy-start(bf16[2048,128]{1,0:T(8,128)(2,1)} %copy-done.4) | copy-start | bytes 1572868
  853.9 19.1 %copy-start.7 = (bf16[2048,128]{1,0:T(8,128)(2,1)S(1)}, bf16[2048,128]{1,0:T(8,128)(2,1)}, u32[]{:S(2)}) copy-start(bf16[2048,128]{1,0:T(8,128)(2,1)} %copy-done.6) | copy-start | bytes 1572868
  853.9 19.1 %copy-start.12 = (bf16[4,512,2,128]{3,1,2,0:T(8,128)(2,1)S(1)}, bf16[4,512,2,128]{3,1,2,0:T(8,128)(2,1)}, u32[]{:S(2)}) copy-start(bf16[4,512,2,128]{3,1,2,0:T(8,128)(2,1)} %copy-done.11) | copy-start | bytes 3145732
  1005.9 187.3 %copy-start.53 = (f32[64]{0:T(128)S(1)}, f32[64]{0:T(128)}, u32[]{:S(2)}) copy-start(f32[64]{0:T(128)} %copy-done.52) | copy-start | bytes 772
  1005.9 187.6 %copy-start.10 = (bf16[256,2048]{0,1:T(8,128)(2,1)S(1)}, bf16[256,2048]{0,1:T(8,128)(2,1)}, u32[]{:S(2)}) copy-start(bf16[256,2048]{0,1:T(8,128)(2,1)} %fusion.50) | copy-start | bytes 3145732
  1005.9 261.8 %reduce-scatter.19.cloned.1.call-start = ((), (), s32[]{:S(2)}) async-start(), calls=%async_computation.25 | async-start | bytes 1310720 | tf_op jit(solution)/shard_map/reduce_scatter | solution.py:273
  1194.9 72.7 %reduce-scatter.21.cloned.1.call-start = ((), (), s32[]{:S(2)}) async-start(), calls=%async_computation.26 | async-start | bytes 1310720 | tf_op jit(solution)/shard_map/reduce_scatter | solution.py:274
  1196.4 226.1 %reduce-scatter.11.cloned.1.call-start = ((), (), s32[]{:S(2)}) async-start(), calls=%async_computation.19 | async-start | bytes 18874368 | tf_op jit(solution)/shard_map/reduce_scatter | solution.py:208
  1209.2 281.2 %reduce-scatter.29.cloned.1.call-start = ((), (), s32[]{:S(2)}) async-start(), calls=%async_computation.30 | async-start | bytes 7208960 | tf_op jit(solution)/shard_map/reduce_scatter | solution.py:279
  1220.4 339.1 %reduce-scatter.25.cloned.1.call-start = ((), (), s32[]{:S(2)}) async-start(), calls=%async_computation.28 | async-start | bytes 7208960 | tf_op jit(solution)/shard_map/reduce_scatter | solution.py:277
  1231.7 396.9 %reduce-scatter.27.cloned.1.call-start = ((), (), s32[]{:S(2)}) async-start(), calls=%async_computation.29 | async-start | bytes 7208960 | tf_op jit(solution)/shard_map/reduce_scatter | solution.py:278
  1243.0 424.5 %reduce-scatter.17.cloned.1.call-start = ((), (), s32[]{:S(2)}) async-start(), calls=%async_computation.24 | async-start | bytes 2621440 | tf_op jit(solution)/shard_map/reduce_scatter | solution.py:272
  1250.5 455.5 %reduce-scatter.23.cloned.1.call-start = ((), (), s32[]{:S(2)}) async-start(), calls=%async_computation.27 | async-start | bytes 2621440 | tf_op jit(solution)/shard_map/reduce_scatter | solution.py:275
  1260.1 505.0 %all-reduce.7.cloned.1.call-start = ((), (), s32[]{:S(2)}) async-start(), calls=%async_computation.31 | async-start | bytes 1048576 | tf_op jit(solution)/shard_map/psum | solution.py:281
  1264.3 158.3 %copy-start.1 = (f32[256,2048]{0,1:T(8,128)S(1)}, f32[256,2048]{0,1:T(8,128)}, u32[]{:S(2)}) copy-start(f32[256,2048]{0,1:T(8,128)} %copy-done) | copy-start | bytes 6291460
  1264.3 158.2 %copy-start.35 = (f32[4,1,512]{2,1,0:T(1,128)S(1)}, f32[4,1,512]{2,1,0:T(1,128)}, u32[]{:S(2)}) copy-start(f32[4,1,512]{2,1,0:T(1,128)} %copy-done.34) | copy-start | bytes 24580
  1264.3 158.2 %copy-start.46 = (f32[256]{0:T(256)S(1)}, f32[256]{0:T(256)}, u32[]{:S(2)}) copy-start(f32[256]{0:T(256)} %copy-done.45) | copy-start | bytes 3076
  1264.3 158.2 %copy-start.50 = (f32[256]{0:T(256)S(1)}, f32[256]{0:T(256)}, u32[]{:S(2)}) copy-start(f32[256]{0:T(256)} %copy-done.49) | copy-start | bytes 3076
  1427.5 20.2 %copy-start.20 = (bf16[256,2048]{0,1:T(8,128)(2,1)S(1)}, bf16[256,2048]{0,1:T(8,128)(2,1)}, u32[]{:S(2)}) copy-start(bf16[256,2048]{0,1:T(8,128)(2,1)} %get-tuple-element.384) | copy-start | bytes 3145732
  (41 other events, 227.1 us)
Sparse Core Ops, SparseCore 0:
  10.4 29.0 all-gather.16
  41.7 82.4 all-gather.12
  126.6 24.6 all-gather.14
  152.8 82.0 all-gather.18
  236.5 40.0 all-gather.22
  304.8 80.4 all-gather.20
  387.7 39.7 all-gather.24
  429.3 41.5 all-gather.26
  472.4 82.0 all-gather.28
  594.2 166.6 reduce-scatter.12
  765.8 80.9 all-gather.30
  1006.0 186.0 reduce-scatter.14
  1195.0 26.3 reduce-scatter.18
  1224.2 27.9 reduce-scatter.20
  1254.4 168.1 reduce-scatter.10
  1426.0 64.4 reduce-scatter.28
  1493.8 65.6 reduce-scatter.24
  1563.0 65.6 reduce-scatter.26
  1632.2 35.1 reduce-scatter.16
  1670.8 35.1 reduce-scatter.22
  1708.4 56.5 all-reduce.6
where the time goes:
time: 1780 us
  waiting for transfers between devices  1180 us (66%)
  matrix products  230 us (13%)
  local copies, waits for them, and re-layouts  159 us (9%)
  other arithmetic  96.3 us (5%)
  blocking collectives  68.7 us (4%)
    reduce_scatter x1, waiting for transfers between devices, local(): lax.psum_scatter(grad_parts, 'col', scatter_dimension=0, tiled=True)  184 us
    reduce_scatter x1, waiting for transfers between devices, local(): lax.psum_scatter(jnp.dot(gate_grad, gate_copy.T, preferred_element_type=j...  165 us
    reduce_scatter x1, waiting for transfers between devices, local(): lax.psum_scatter(jnp.dot(hidden, down_copy, preferred_element_type=jnp.fl...  155 us
    all_gather x1, waiting for transfers between devices, local(): lax.all_gather(out_grad, 'col', axis=0, tiled=True)  83.7 us
    all_gather x1, waiting for transfers between devices, local(): middle_rows = lax.all_gather(middle_low, 'col', axis=0, tiled=True)  81 us
    all_gather x1, waiting for transfers between devices, local(): lax.all_gather(normed_two.astype(jnp.bfloat16), 'col', axis=0, tiled=True)  74.6 us
    reduce_scatter x1, waiting for transfers between devices, local(): lax.psum_scatter(up_wgrad, 'row', scatter_dimension=0, tiled=True)  69.1 us
    reduce_scatter x1, waiting for transfers between devices, local(): lax.psum_scatter(gate_wgrad, 'row', scatter_dimension=0, tiled=True)  69.1 us
  transfers between devices with their start and end apart: 22, of which 18 were waited for; matrix products, arithmetic and copies ran while one was open for 16% of the time, Pallas kernels for 0%

commit v1 on v0

--- a/solution.py
+++ b/solution.py
@@ -6,6 +6,19 @@
 norm_eps = 1e-05
 rope_base = 10000.0
 masked_score = -1e30
+
+
+def ring_gather(value, axis, dim):
+    ways = lax.axis_size(axis)
+    up = [(d, (d + 1) % ways) for d in range(ways)]
+    down = [(d, (d - 1) % ways) for d in range(ways)]
+    earlier, later = ([value], [value])
+    for _ in range(ways // 2):
+        earlier.append(lax.ppermute(earlier[-1], axis, up))
+    for _ in range((ways - 1) // 2):
+        later.append(lax.ppermute(later[-1], axis, down))
+    line = jnp.concatenate([*earlier[::-1], *later[1:]], axis=dim)
+    return jnp.roll(line, (lax.axis_index(axis) - ways // 2) * value.shape[dim], axis=dim)
 
 
 def rotate_pairs(values, positions, direction):
@@ -229,7 +242,7 @@
     middle_part, gain_two_grad = norm_backward(middle, factor_two, gain_two, normed_two_grad)
     middle_grad = out_grad.astype(jnp.float32) + middle_part
     middle_low = middle_grad.astype(jnp.bfloat16)
-    middle_rows = lax.all_gather(middle_low, "col", axis=0, tiled=True)
+    middle_rows = ring_gather(middle_low, "col", 0)
     mixed_grad_slot = jnp.dot(middle_rows, out_copy.T, preferred_element_type=jnp.float32).astype(
         jnp.bfloat16
     )

time: 1780 us -> 1800 us (1.011)
    all_gather x1 -> x0, waiting for transfers between devices: 81 us -> none  [local(): middle_rows = lax.all_gather(middle_low, 'col', axis=0, tiled=True)]
    ppermute x0 -> x7, waiting for transfers between devices: none -> 77.7 us  [the longest x4 77.6 us: ring_gather(): earlier.append(lax.ppermute(earlier[-1], axis, up))]
    unnamed x133 -> x160, local copies, waits for them, and re-layouts: 23.7 us -> 36.3 us
  transfers between devices with their start and end apart: 22 -> 28, of which waited for: 18 -> 22; matrix products, arithmetic and copies ran while one was open for 16% -> 16% of each run, Pallas kernels for 0% -> 0%
where the time goes in v1:
time: 1800 us; the launch traced here: 1790 us
  waiting for transfers between devices  1180 us (66%)
  matrix products  226 us (13%)
  local copies, waits for them, and re-layouts  172 us (10%)
  other arithmetic  95.6 us (5%)
  blocking collectives  68.6 us (4%)
    reduce_scatter x1, waiting for transfers between devices, local(): lax.psum_scatter(grad_parts, 'col', scatter_dimension=0, tiled=True)  184 us
    reduce_scatter x1, waiting for transfers between devices, local(): lax.psum_scatter(jnp.dot(gate_grad, gate_copy.T, preferred_element_type=j...  165 us
    reduce_scatter x1, waiting for transfers between devices, local(): lax.psum_scatter(jnp.dot(hidden, down_copy, preferred_element_type=jnp.fl...  155 us
    all_gather x1, waiting for transfers between devices, local(): lax.all_gather(out_grad, 'col', axis=0, tiled=True)  83.7 us
    ppermute x4, waiting for transfers between devices, ring_gather(): earlier.append(lax.ppermute(earlier[-1], axis, up))  77.6 us
    all_gather x1, waiting for transfers between devices, local(): lax.all_gather(normed_two.astype(jnp.bfloat16), 'col', axis=0, tiled=True)  74.5 us
    reduce_scatter x1, waiting for transfers between devices, local(): lax.psum_scatter(gate_wgrad, 'row', scatter_dimension=0, tiled=True)  69.1 us
    reduce_scatter x1, waiting for transfers between devices, local(): lax.psum_scatter(up_wgrad, 'row', scatter_dimension=0, tiled=True)  69.1 us
  transfers between devices with their start and end apart: 28, of which 22 were waited for; matrix products, arithmetic and copies ran while one was open for 16% of the time, Pallas kernels for 0%

profile of v1, /device:TPU:0, one launch (start us, length us, event | category | flops | bytes accessed | tf_op | source)
XLA Modules:
  0.0 1791.2 jit_solution(1505286798181201733)
XLA Ops:
  9.8 9.6 all-gather
  24.1 15.4 all-gather.16.cloned.1.call-done
  40.9 8.0 scatter_custom_fusion
  49.1 11.8 gather_fusion
  61.0 10.1 all_gather.43
  71.1 9.6 all_gather.42
  86.5 37.7 %all-gather.12.cloned.1.call-done = bf16[2048,2048]{0,1:T(8,128)(2,1)} async-done(((bf16[256,2048]{0,1:T(8,128)(2,1)}), bf16[2048,2048]{0,1:T(8,128)(2,1)}) %all-gather.12.cloned.1.call-update) | async-done | bytes 8388624 | tf_op jit(solution)/shard_map/all_gather | solution.py:191
  173.7 13.9 gather_fusion.1
  189.1 50.7 %while.27 = (s32[]{:T(128)}, bf16[4,512,2,128]{3,1,0,2:T(8,128)(2,1)}, f32[4,2,512]{2,1,0:T(2,128)S(1)}, s32[4]{0:T(128)S(1)}, s32[2048]{0:T(1024)S(1)}, /*index...) while((s32[]{:T(128)}, ...), condition=%wide.region_8.9_spmd, body=%wide.region_5.8_spmd.sunk | while | flops 1102183936 | bytes 30984376 | solution.py:93
  243.8 15.1 gather_fusion.4
  268.4 8.2 all-gather.1
  276.7 18.3 %all-to-all-done = bf16[8,256,256]{1,2,0:T(8,128)(2,1)S(1)} async-done(((bf16[8,256,256]{1,2,0:T(8,128)(2,1)}), bf16[8,256,256]{1,2,0:T(8,128)(2,1)S(1)}, u32[]{:S(2)}, u32[]{:S(2)}) %all-to-all-start) | async-done | bytes 1048608 | tf_op jit(solution)/shard_map/all_to_all | solution.py:211
  310.9 74.5 %all-gather.20.cloned.1.call-done = bf16[2048,2048]{0,1:T(8,128)(2,1)} async-done(((bf16[256,2048]{0,1:T(8,128)(2,1)}), bf16[2048,2048]{0,1:T(8,128)(2,1)}) %all-gather.20.cloned.1.call-update) | async-done | bytes 8388624 | tf_op jit(solution)/shard_map/all_gather | solution.py:215
  385.4 11.1 fusion.107
  396.5 31.1 %all-gather.24.cloned.1.call-done = bf16[2048,704]{0,1:T(8,128)(2,1)} async-done(((bf16[512,704]{0,1:T(8,128)(2,1)}), bf16[2048,704]{0,1:T(8,128)(2,1)}) %all-gather.24.cloned.1.call-update) | async-done | bytes 2883600 | tf_op jit(solution)/shard_map/all_gather | solution.py:176
  427.6 11.1 fusion.108
  438.6 32.3 %all-gather.26.cloned.1.call-done = bf16[704,2048]{1,0:T(8,128)(2,1)} async-done(((bf16[704,512]{1,0:T(8,128)(2,1)}), bf16[704,2048]{1,0:T(8,128)(2,1)}) %all-gather.26.cloned.1.call-update) | async-done | bytes 2883600 | tf_op jit(solution)/shard_map/all_gather | solution.py:177
  471.0 83.7 %all-gather.28.cloned.1.call-done = bf16[2048,2048]{1,0:T(8,128)(2,1)} async-done(((bf16[256,2048]{1,0:T(8,128)(2,1)}), bf16[2048,2048]{1,0:T(8,128)(2,1)}) %all-gather.28.cloned.1.call-update) | async-done | bytes 8388624 | tf_op jit(solution)/shard_map/all_gather | solution.py:192
  554.6 15.3 multiply_convert_fusion
  569.9 10.4 fusion.103
  580.4 13.9 convolution_add_fusion
  595.8 165.3 %reduce-scatter.13.cloned.1.call-done = f32[256,2048]{0,1:T(8,128)} async-done(((f32[2048,2048]{0,1:T(8,128)}), f32[256,2048]{0,1:T(8,128)}) %reduce-scatter.13.cloned.1.call-update) | async-done | bytes 2097168 | tf_op jit(solution)/shard_map/reduce_scatter | solution.py:235
  764.9 16.0 collective-permute-done
  784.5 21.4 %collective-permute-done.1 = bf16[256,2048]{0,1:T(8,128)(2,1)S(1)} collective-permute-done((bf16[256,2048]{0,1:T(8,128)(2,1)S(1)}, bf16[256,2048]{0,1:T(8,128)(2,1)S(1)}, u32[]{:S(2)}, u32[]{:S(2)}) %collective-permute-start.1) | collective-permute-done | bytes 1048608 | tf_op jit(solution)/shard_map/ppermute | solution.py:17
  809.5 20.2 %collective-permute-done.2 = bf16[256,2048]{0,1:T(8,128)(2,1)} collective-permute-done((bf16[256,2048]{0,1:T(8,128)(2,1)S(1)}, bf16[256,2048]{0,1:T(8,128)(2,1)}, u32[]{:S(2)}, u32[]{:S(2)}) %collective-permute-start.2) | collective-permute-done | bytes 1048608 | tf_op jit(solution)/shard_map/ppermute | solution.py:17
  833.6 20.0 %collective-permute-done.3 = bf16[256,2048]{0,1:T(8,128)(2,1)} collective-permute-done((bf16[256,2048]{0,1:T(8,128)(2,1)}, bf16[256,2048]{0,1:T(8,128)(2,1)}, u32[]{:S(2)}, u32[]{:S(2)}) %collective-permute-start.3) | collective-permute-done | bytes 1048608 | tf_op jit(solution)/shard_map/ppermute | solution.py:17
  873.5 15.0 gather_fusion.5
  888.5 77.5 %while.28 = (s32[]{:T(128)}, f32[2048,128]{1,0:T(8,128)S(1)}, f32[2048,128]{1,0:T(8,128)}, f32[4,512,2,128]{3,1,0,2:T(8,128)}, s32[4]{0:T(128)S(1)}, /*index=5*/...) while((s32[]{:T(128)}, f32[2048,128]{1,0:T(8,128)S(1)}, ...), condition=%wide.region_15.16_spmd.clone, body=%wide.region_13.15_spmd.clone.sunk | while | flops 2720398848 | bytes 83409176 | solution.py:132
  970.9 14.6 gather_fusion.6
  986.9 8.6 gather_fusion.7
  998.5 9.0 subtract_convert_fusion
  1012.8 8.8 pad_maximum_fusion
  1023.4 184.4 %reduce-scatter.15.cloned.1.call-done = f32[256,2304]{0,1:T(8,128)} async-done(((f32[2048,2304]{0,1:T(8,128)}), f32[256,2304]{0,1:T(8,128)}) %reduce-scatter.15.cloned.1.call-update) | async-done | bytes 2359312 | tf_op jit(solution)/shard_map/reduce_scatter | solution.py:265
  1212.1 12.7 fusion.102
  1224.9 11.1 fusion.106
  1236.1 11.2 fusion.104
  1247.4 11.1 fusion.105
  1258.8 7.2 fusion.66
  1268.1 7.5 fusion.47
  1283.1 155.2 %reduce-scatter.11.cloned.1.call-done = f32[256,2048]{0,1:T(8,128)} async-done(((f32[2048,2048]{0,1:T(8,128)}), f32[256,2048]{0,1:T(8,128)}) %reduce-scatter.11.cloned.1.call-update) | async-done | bytes 2097168 | tf_op jit(solution)/shard_map/reduce_scatter | solution.py:221
  1443.3 17.1 all-reduce.4
  1464.9 14.1 all-reduce.2
  1479.0 27.2 %reduce-scatter.29.cloned.1.call-done = f32[704,512]{1,0:T(8,128)} async-done(((f32[704,2048]{1,0:T(8,128)}), f32[704,512]{1,0:T(8,128)}) %reduce-scatter.29.cloned.1.call-update) | async-done | bytes 1441808 | tf_op jit(solution)/shard_map/reduce_scatter | solution.py:292
  1506.3 69.1 %reduce-scatter.25.cloned.1.call-done = f32[512,704]{0,1:T(8,128)} async-done(((f32[2048,704]{0,1:T(8,128)}), f32[512,704]{0,1:T(8,128)}) %reduce-scatter.25.cloned.1.call-update) | async-done | bytes 1441808 | tf_op jit(solution)/shard_map/reduce_scatter | solution.py:290
  1575.4 69.1 %reduce-scatter.27.cloned.1.call-done = f32[512,704]{0,1:T(8,128)} async-done(((f32[2048,704]{0,1:T(8,128)}), f32[512,704]{0,1:T(8,128)}) %reduce-scatter.27.cloned.1.call-update) | async-done | bytes 1441808 | tf_op jit(solution)/shard_map/reduce_scatter | solution.py:291
  1644.5 38.6 %reduce-scatter.17.cloned.1.call-done = f32[512,256]{1,0:T(8,128)} async-done(((f32[2048,256]{1,0:T(8,128)}), f32[512,256]{1,0:T(8,128)}) %reduce-scatter.17.cloned.1.call-update) | async-done | bytes 524304 | tf_op jit(solution)/shard_map/reduce_scatter | solution.py:285
  1683.1 38.8 %reduce-scatter.23.cloned.1.call-done = f32[256,512]{1,0:T(8,128)} async-done(((f32[256,2048]{1,0:T(8,128)}), f32[256,512]{1,0:T(8,128)}) %reduce-scatter.23.cloned.1.call-update) | async-done | bytes 524304 | tf_op jit(solution)/shard_map/reduce_scatter | solution.py:288
  1721.9 58.9 %all-reduce.7.cloned.1.call-done = (f32[512,128]{1,0:T(8,128)}, f32[512,128]{1,0:T(8,128)}) async-done(((f32[512,128]{1,0:T(8,128)}, f32[512,128]{1,0:T(8,128)}), (f32[512,128]{1,0:T(8,128)}, f32[512,128]{1,0:T(8,128)})) %all-reduce.7.cloned.1.call-update) | async-done | bytes 524304 | tf_op jit(solution)/shard_map/psum | solution.py:294
  (384 shorter events, 285.4 us)
Async XLA Ops:
  7.2 32.3 %all-gather.16.cloned.1.call-start = ((), (), s32[]{:S(2)}) async-start(), calls=%async_computation.13 | async-start | bytes 1310720 | tf_op jit(solution)/shard_map/all_gather | solution.py:173
  9.1 115.1 %all-gather.12.cloned.1.call-start = ((), (), s32[]{:S(2)}) async-start(), calls=%async_computation.11 | async-start | bytes 9437184 | tf_op jit(solution)/shard_map/all_gather | solution.py:191
  21.0 274.9 %copy-start.2 = (bf16[256,2048]{0,1:T(8,128)(2,1)}, bf16[256,2048]{0,1:T(8,128)(2,1)S(1)}, u32[]{:S(2)}) copy-start(bf16[256,2048]{0,1:T(8,128)(2,1)S(1)} %copy.114) | copy-start | bytes 3145732
  23.3 128.0 %all-gather.14.cloned.1.call-start = ((), (), s32[]{:S(2)}) async-start(), calls=%async_computation.12 | async-start | bytes 1310720 | tf_op jit(solution)/shard_map/all_gather | solution.py:170
  24.1 252.6 %all-gather.18.cloned.1.call-start = ((), (), s32[]{:S(2)}) async-start(), calls=%async_computation.14 | async-start | bytes 9437184 | tf_op jit(solution)/shard_map/all_gather | solution.py:210
  39.6 271.3 %all-gather.22.cloned.1.call-start = ((), (), s32[]{:S(2)}) async-start(), calls=%async_computation.16 | async-start | bytes 3604480 | tf_op jit(solution)/shard_map/all_gather | solution.py:175
  40.6 93.5 %copy-start.58 = (f32[64]{0:T(128)}, f32[64]{0:T(128)S(1)}, u32[]{:S(2)}) copy-start(f32[64]{0:T(128)S(1)} %multiply_power_fusion) | copy-start | bytes 772
  48.9 124.8 %copy-start.41 = (s32[2048]{0:T(1024)}, s32[2048]{0:T(1024)S(1)}, u32[]{:S(2)}) copy-start(s32[2048]{0:T(1024)S(1)} %fusion.92) | copy-start | bytes 24580
  49.1 194.7 %copy-start.43 = (s32[2048]{0:T(1024)}, s32[2048]{0:T(1024)S(1)}, u32[]{:S(2)}) copy-start(s32[2048]{0:T(1024)S(1)} %get-tuple-element.398) | copy-start | bytes 24580
  60.9 68.0 %copy-start.49 = (s32[2048]{0:T(1024)}, s32[2048]{0:T(1024)S(1)}, u32[]{:S(2)}) copy-start(s32[2048]{0:T(1024)S(1)} %gather_fusion) | copy-start | bytes 24580
  71.1 53.1 %copy-start.29 = (bf16[2048,128]{1,0:T(8,128)(2,1)}, bf16[2048,128]{1,0:T(8,128)(2,1)S(1)}, u32[]{:S(2)}) copy-start(bf16[2048,128]{1,0:T(8,128)(2,1)S(1)} %all_gather.43) | copy-start | bytes 1572868
  80.6 48.6 %copy-start.25 = (bf16[2048,128]{1,0:T(8,128)(2,1)}, bf16[2048,128]{1,0:T(8,128)(2,1)S(1)}, u32[]{:S(2)}) copy-start(bf16[2048,128]{1,0:T(8,128)(2,1)S(1)} %all_gather.42) | copy-start | bytes 1572868
  263.7 31.2 %all-to-all-start = ((bf16[8,256,256]{1,2,0:T(8,128)(2,1)}), bf16[8,256,256]{1,2,0:T(8,128)(2,1)S(1)}, u32[]{:S(2)}, u32[]{:S(2)}) async-start(bf16[8,256,256]{1,2,0:T(8,128)(2,1)} %copy.124), calls=%async_computation | async-start | bytes 2097152 | tf_op jit(solution)/shard_map/all_to_all | solution.py:211
  268.4 117.0 %all-gather.20.cloned.1.call-start = ((), (), s32[]{:S(2)}) async-start(), calls=%async_computation.15 | async-start | bytes 9437184 | tf_op jit(solution)/shard_map/all_gather | solution.py:215
  276.6 487.5 %copy-start.39 = (f32[4,1,512]{2,1,0:T(1,128)}, f32[4,1,512]{2,1,0:T(1,128)S(1)}, u32[]{:S(2)}) copy-start(f32[4,1,512]{2,1,0:T(1,128)S(1)} %convert_element_type.144) | copy-start | bytes 24580
  303.0 461.1 %copy-start = (f32[256,2048]{0,1:T(8,128)}, f32[256,2048]{0,1:T(8,128)S(1)}, u32[]{:S(2)}) copy-start(f32[256,2048]{0,1:T(8,128)S(1)} %get-tuple-element.395) | copy-start | bytes 6291460
  303.0 461.1 %copy-start.51 = (f32[256]{0:T(256)}, f32[256]{0:T(256)S(1)}, u32[]{:S(2)}) copy-start(f32[256]{0:T(256)S(1)} %add_rsqrt_fusion) | copy-start | bytes 3076
  304.8 122.8 %all-gather.24.cloned.1.call-start = ((), (), s32[]{:S(2)}) async-start(), calls=%async_computation.17 | async-start | bytes 3604480 | tf_op jit(solution)/shard_map/all_gather | solution.py:176
  307.2 163.8 %all-gather.26.cloned.1.call-start = ((), (), s32[]{:S(2)}) async-start(), calls=%async_computation.18 | async-start | bytes 3604480 | tf_op jit(solution)/shard_map/all_gather | solution.py:177
  310.0 244.6 %all-gather.28.cloned.1.call-start = ((), (), s32[]{:S(2)}) async-start(), calls=%async_computation.20 | async-start | bytes 9437184 | tf_op jit(solution)/shard_map/all_gather | solution.py:192
  310.8 450.3 %reduce-scatter.13.cloned.1.call-start = ((), (), s32[]{:S(2)}) async-start(), calls=%async_computation.21 | async-start | bytes 18874368 | tf_op jit(solution)/shard_map/reduce_scatter | solution.py:235
  594.3 613.5 %reduce-scatter.15.cloned.1.call-start = ((), (), s32[]{:S(2)}) async-start(), calls=%async_computation.22 | async-start | bytes 21233664 | tf_op jit(solution)/shard_map/reduce_scatter | solution.py:265
  595.8 169.0 %copy-start.14 = (bf16[256,2048]{0,1:T(8,128)(2,1)}, bf16[256,2048]{0,1:T(8,128)(2,1)S(1)}, u32[]{:S(2)}) copy-start(bf16[256,2048]{0,1:T(8,128)(2,1)S(1)} %copy.127) | copy-start | bytes 3145732
  764.1 90.8 %copy-start.55 = (f32[256]{0:T(256)}, f32[256]{0:T(256)S(1)}, u32[]{:S(2)}) copy-start(f32[256]{0:T(256)S(1)} %broadcast_multiply_fusion.2) | copy-start | bytes 3076
  764.9 16.1 collective-permute-start
  780.9 25.0 %collective-permute-start.1 = (bf16[256,2048]{0,1:T(8,128)(2,1)S(1)}, bf16[256,2048]{0,1:T(8,128)(2,1)S(1)}, u32[]{:S(2)}, u32[]{:S(2)}) collective-permute-start(bf16[256,2048]{0,1:T(8,128)(2,1)S(1)} %collective-permute-done), channel_id=1, source_target_pairs={{0,1},{1,2},{2,3},{3,4},{4,5},{5,6},{6,7},{7,0},{8,9},{9,10},{10,1... | collective-permute-start | bytes 3145736 | tf_op jit(solution)/shard_map/ppermute | solution.py:17
  780.9 25.0 %collective-permute-start.4 = (bf16[256,2048]{0,1:T(8,128)(2,1)S(1)}, bf16[256,2048]{0,1:T(8,128)(2,1)S(1)}, u32[]{:S(2)}, u32[]{:S(2)}) collective-permute-start(bf16[256,2048]{0,1:T(8,128)(2,1)S(1)} %fusion.99), channel_id=1, source_target_pairs={{0,7},{1,0},{2,1},{3,2},{4,3},{5,4},{6,5},{7,6},{8,15},{9,8},{10,9... | collective-permute-start | bytes 3145736 | tf_op jit(solution)/shard_map/ppermute | solution.py:19
  805.9 23.8 %collective-permute-start.2 = (bf16[256,2048]{0,1:T(8,128)(2,1)S(1)}, bf16[256,2048]{0,1:T(8,128)(2,1)}, u32[]{:S(2)}, u32[]{:S(2)}) collective-permute-start(bf16[256,2048]{0,1:T(8,128)(2,1)S(1)} %collective-permute-done.1), channel_id=1, source_target_pairs={{0,1},{1,2},{2,3},{3,4},{4,5},{5,6},{6,7},{7,0},{8,9},{9,10},{10,1... | collective-permute-start | bytes 3145736 | tf_op jit(solution)/shard_map/ppermute | solution.py:17
  806.9 22.9 %collective-permute-start.5 = (bf16[256,2048]{0,1:T(8,128)(2,1)S(1)}, bf16[256,2048]{0,1:T(8,128)(2,1)}, u32[]{:S(2)}, u32[]{:S(2)}) collective-permute-start(bf16[256,2048]{0,1:T(8,128)(2,1)S(1)} %collective-permute-done.4), channel_id=1, source_target_pairs={{0,7},{1,0},{2,1},{3,2},{4,3},{5,4},{6,5},{7,6},{8,15},{9,8},{10,9... | collective-permute-start | bytes 3145736 | tf_op jit(solution)/shard_map/ppermute | solution.py:19
  829.7 23.9 %collective-permute-start.3 = (bf16[256,2048]{0,1:T(8,128)(2,1)}, bf16[256,2048]{0,1:T(8,128)(2,1)}, u32[]{:S(2)}, u32[]{:S(2)}) collective-permute-start(bf16[256,2048]{0,1:T(8,128)(2,1)} %collective-permute-done.2), channel_id=1, source_target_pairs={{0,1},{1,2},{2,3},{3,4},{4,5},{5,6},{6,7},{7,0},{8,9},{9,10},{10,1... | collective-permute-start | bytes 3145736 | tf_op jit(solution)/shard_map/ppermute | solution.py:17
  829.7 26.6 %copy-start.24 = (bf16[256,2048]{0,1:T(8,128)(2,1)S(1)}, bf16[256,2048]{0,1:T(8,128)(2,1)}, u32[]{:S(2)}) copy-start(bf16[256,2048]{0,1:T(8,128)(2,1)} %copy-done.23) | copy-start | bytes 3145732
  829.7 26.9 %copy-start.16 = (bf16[256,2048]{0,1:T(8,128)(2,1)S(1)}, bf16[256,2048]{0,1:T(8,128)(2,1)}, u32[]{:S(2)}) copy-start(bf16[256,2048]{0,1:T(8,128)(2,1)} %copy-done.15) | copy-start | bytes 3145732
  829.8 28.5 %collective-permute-start.6 = (bf16[256,2048]{0,1:T(8,128)(2,1)}, bf16[256,2048]{0,1:T(8,128)(2,1)S(1)}, u32[]{:S(2)}, u32[]{:S(2)}) collective-permute-start(bf16[256,2048]{0,1:T(8,128)(2,1)} %collective-permute-done.5), channel_id=1, source_target_pairs={{0,7},{1,0},{2,1},{3,2},{4,3},{5,4},{6,5},{7,6},{8,15},{9,8},{10,9... | collective-permute-start | bytes 3145736 | tf_op jit(solution)/shard_map/ppermute | solution.py:19
  1021.6 187.2 %copy-start.59 = (f32[64]{0:T(128)S(1)}, f32[64]{0:T(128)}, u32[]{:S(2)}) copy-start(f32[64]{0:T(128)} %copy-done.58) | copy-start | bytes 772
  1021.6 187.5 %copy-start.10 = (bf16[256,2048]{0,1:T(8,128)(2,1)S(1)}, bf16[256,2048]{0,1:T(8,128)(2,1)}, u32[]{:S(2)}) copy-start(bf16[256,2048]{0,1:T(8,128)(2,1)} %fusion.57) | copy-start | bytes 3145732
  1021.6 261.5 %reduce-scatter.19.cloned.1.call-start = ((), (), s32[]{:S(2)}) async-start(), calls=%async_computation.24 | async-start | bytes 1310720 | tf_op jit(solution)/shard_map/reduce_scatter | solution.py:286
  1210.6 72.5 %reduce-scatter.21.cloned.1.call-start = ((), (), s32[]{:S(2)}) async-start(), calls=%async_computation.25 | async-start | bytes 1310720 | tf_op jit(solution)/shard_map/reduce_scatter | solution.py:287
  1212.1 226.3 %reduce-scatter.11.cloned.1.call-start = ((), (), s32[]{:S(2)}) async-start(), calls=%async_computation.19 | async-start | bytes 18874368 | tf_op jit(solution)/shard_map/reduce_scatter | solution.py:221
  1224.9 281.4 %reduce-scatter.29.cloned.1.call-start = ((), (), s32[]{:S(2)}) async-start(), calls=%async_computation.29 | async-start | bytes 7208960 | tf_op jit(solution)/shard_map/reduce_scatter | solution.py:292
  1236.0 339.3 %reduce-scatter.25.cloned.1.call-start = ((), (), s32[]{:S(2)}) async-start(), calls=%async_computation.27 | async-start | bytes 7208960 | tf_op jit(solution)/shard_map/reduce_scatter | solution.py:290
  1247.3 397.2 %reduce-scatter.27.cloned.1.call-start = ((), (), s32[]{:S(2)}) async-start(), calls=%async_computation.28 | async-start | bytes 7208960 | tf_op jit(solution)/shard_map/reduce_scatter | solution.py:291
  1258.5 424.6 %reduce-scatter.17.cloned.1.call-start = ((), (), s32[]{:S(2)}) async-start(), calls=%async_computation.23 | async-start | bytes 2621440 | tf_op jit(solution)/shard_map/reduce_scatter | solution.py:285
  1266.0 455.9 %reduce-scatter.23.cloned.1.call-start = ((), (), s32[]{:S(2)}) async-start(), calls=%async_computation.26 | async-start | bytes 2621440 | tf_op jit(solution)/shard_map/reduce_scatter | solution.py:288
  1275.6 505.1 %all-reduce.7.cloned.1.call-start = ((), (), s32[]{:S(2)}) async-start(), calls=%async_computation.30 | async-start | bytes 1048576 | tf_op jit(solution)/shard_map/psum | solution.py:294
  1279.8 158.6 %copy-start.1 = (f32[256,2048]{0,1:T(8,128)S(1)}, f32[256,2048]{0,1:T(8,128)}, u32[]{:S(2)}) copy-start(f32[256,2048]{0,1:T(8,128)} %copy-done) | copy-start | bytes 6291460
  1279.8 158.6 %copy-start.40 = (f32[4,1,512]{2,1,0:T(1,128)S(1)}, f32[4,1,512]{2,1,0:T(1,128)}, u32[]{:S(2)}) copy-start(f32[4,1,512]{2,1,0:T(1,128)} %copy-done.39) | copy-start | bytes 24580
  1279.8 158.6 %copy-start.52 = (f32[256]{0:T(256)S(1)}, f32[256]{0:T(256)}, u32[]{:S(2)}) copy-start(f32[256]{0:T(256)} %copy-done.51) | copy-start | bytes 3076
  1279.8 158.6 %copy-start.56 = (f32[256]{0:T(256)S(1)}, f32[256]{0:T(256)}, u32[]{:S(2)}) copy-start(f32[256]{0:T(256)} %copy-done.55) | copy-start | bytes 3076
  (53 other events, 497.6 us)
Sparse Core Ops, SparseCore 0:
  10.4 29.0 all-gather.15
  41.7 82.4 all-gather.11
  126.6 24.6 all-gather.13
  152.8 82.0 all-gather.17
  236.5 40.0 all-gather.21
  304.9 80.4 all-gather.19
  387.8 39.7 all-gather.23
  429.4 41.5 all-gather.25
  472.6 82.0 all-gather.27
  594.4 166.6 reduce-scatter.12
  1021.7 186.0 reduce-scatter.14
  1210.7 26.4 reduce-scatter.18
  1240.0 27.8 reduce-scatter.20
  1270.2 168.1 reduce-scatter.10
  1441.8 64.4 reduce-scatter.28
  1509.7 65.6 reduce-scatter.24
  1578.8 65.6 reduce-scatter.26
  1647.9 35.1 reduce-scatter.16
  1686.7 35.1 reduce-scatter.22
  1724.1 56.6 all-reduce.6
